TPU v7x, 32 devices: a whole 2x2x4 slice. The times are simulated.
32 devices in a mesh: level: 2 (over x), subj: 4 (over y, core), gz: 4 (over z).
Axes of the slice: x: 2, y: 2, z: 4, core: 2. Of those that a mesh axis runs over, the one named last changes fastest.
Arguments:
- images: bfloat16 [8, 192, 192, 192], P('subj', 'gz'), may hold values from -6 to 6
- momenta: float32 [8, 96, 3, 96, 96], P('subj', 'gz'), may hold values from -18 to 18
- assign: int32 [8], replicated, may hold values from 0 to 7, as said below
Outputs:
- template: float32 [192, 192, 192], P('gz')
Inputs may be any that keep to these rules, and one draw needn't show every extreme that they name: assign is a permutation of 0 to 7 with assign[i] % 2 == i % 2 for every i.
All inputs are finite; a program needn't handle non-finite values.
Results may differ from a plain program's by a relative error of at most 0.00069.
Values may be sent and summed in bfloat16 or wider, within the bound.
A program may use at most 128 MiB of HBM per device.

v0:
```python
import jax
import jax.numpy as jnp
from jax import lax
from jax.sharding import PartitionSpec as P

SWEEPS = 2


def with_halo(array, sides, width):
    for axis, dim in sides:
        size, length = (lax.axis_size(axis), array.shape[dim])
        up = [(i, (i + 1) % size) for i in range(size - 1)]
        down = [(j, i) for i, j in up]
        last = lax.slice_in_dim(array, length - width, length, axis=dim)
        leading = lax.slice_in_dim(array, 0, width, axis=dim)
        before = lax.ppermute(last, axis, up)
        after = lax.ppermute(leading, axis, down)
        array = jnp.concatenate([before, array, after], axis=dim)
    return array


def band(padded, count, axis):

    def take(offset):
        return lax.slice_in_dim(padded, offset, offset + count, axis=axis)

    return (take(0) + take(4)) * 0.0625 + (take(1) + take(3)) * 0.25 + take(2) * 0.375


def blur_plane(field, axis):
    widths = [(2, 2) if dimension == axis else (0, 0) for dimension in range(field.ndim)]
    return band(jnp.pad(field, widths), field.shape[axis], axis)


def upsample_table(finest, coarse, offset):
    rows_fine = jnp.arange(finest, dtype=jnp.int32)[:, None]
    columns = jnp.arange(coarse, dtype=jnp.int32)[None, :]
    nearest = rows_fine // 2 + offset
    farther = nearest + 2 * (rows_fine % 2) - 1
    return 0.75 * (columns == nearest).astype(jnp.float32) + 0.25 * (columns == farther).astype(
        jnp.float32
    )


def warp_slab(extended, upsampled):
    center = extended[1:-1]
    grad_z = (extended[2:] - extended[:-2]) * 0.5
    padded_y = jnp.pad(center, ((0, 0), (1, 1), (0, 0)))
    grad_y = (padded_y[:, 2:] - padded_y[:, :-2]) * 0.5
    padded_x = jnp.pad(center, ((0, 0), (0, 0), (1, 1)))
    grad_x = (padded_x[:, :, 2:] - padded_x[:, :, :-2]) * 0.5
    return center - (upsampled[:, 0] * grad_x + upsampled[:, 1] * grad_y + upsampled[:, 2] * grad_z)


def relax(extended):
    center = extended[1:-1]
    padded_y = jnp.pad(center, ((0, 0), (1, 1), (0, 0)))
    padded_x = jnp.pad(center, ((0, 0), (0, 0), (1, 1)))
    neighbours = (
        extended[2:]
        + extended[:-2]
        + padded_y[:, 2:]
        + padded_y[:, :-2]
        + padded_x[:, :, 2:]
        + padded_x[:, :, :-2]
    )
    return center + 0.15 * (neighbours - 6.0 * center)


def upsample(velocity_ext, table_xy, table_z):
    highest = lax.Precision.HIGHEST
    section_x = jnp.einsum(
        "zcyx,Xx->zcyX",
        velocity_ext,
        table_xy.astype(jnp.bfloat16),
        preferred_element_type=jnp.float32,
    )
    section_y = jnp.einsum("zcyX,Yy->zcYX", section_x, table_xy, precision=highest)
    return jnp.einsum("zcYX,Zz->ZcYX", section_y, table_z, precision=highest)


def shards(images, momenta, assign):
    count = momenta.shape[0]
    slab = momenta.shape[1]
    coarse = momenta.shape[3]
    finest = images.shape[2]
    fine_slab = images.shape[1]
    level_index = lax.axis_index("level")
    group_index = lax.axis_index("subj")
    zone_index = lax.axis_index("gz")
    table_xy = upsample_table(finest, coarse, 0)
    table_z = upsample_table(fine_slab, slab + 2, 1)
    rim_width = 3
    ticker = 0 + level_index
    weight = (ticker < count).astype(jnp.float32)
    ticker = jnp.minimum(ticker, count - 1)
    moment = lax.dynamic_index_in_dim(momenta, ticker, 0, keepdims=False)
    extended = with_halo(moment, (("gz", 0),), rim_width)
    smooth = blur_plane(blur_plane(extended, 3), 2)
    field = band(smooth, extended.shape[0] - 4, 0)
    global_z = zone_index * slab - 1 + jnp.arange(field.shape[0], dtype=jnp.int32)
    inside = (global_z >= 0) & (global_z < slab * lax.axis_size("gz"))
    field = jnp.where(inside[:, None, None, None], field, 0.0)
    field = field.astype(jnp.bfloat16)
    source = assign[group_index * count + ticker] // count
    piece = lax.all_gather(field[None], "subj", axis=0, tiled=True)
    positions = jnp.arange(piece.shape[0], dtype=jnp.int32)
    matched = (positions == source)[:, None, None, None, None]
    arrived = jnp.sum(jnp.where(matched, piece, jnp.zeros_like(piece)), axis=0)
    image = lax.dynamic_index_in_dim(images, ticker, 0, keepdims=False)
    image_rows = image.reshape(slab, -1)
    extended = with_halo(image_rows, (("gz", 0),), 1)
    image_ext = extended.reshape(2 * slab + 4, finest, finest)[1:-1]
    total = weight * warp_slab(image_ext.astype(jnp.float32), upsample(arrived, table_xy, table_z))
    summed = lax.psum(total, ("level", "subj"))
    mean = summed / (lax.axis_size("subj") * count)
    for repeat in range(SWEEPS):
        mean = relax(with_halo(mean, (("gz", 0),), 1))
    return mean


def solution(mesh):
    return jax.shard_map(
        shards,
        mesh=mesh,
        in_specs=(P("subj", "gz", None, None), P("subj", "gz", None, None, None), P()),
        out_specs=P("gz", None, None),
        check_vma=False,
    )
```

profile of v0, /device:TPU:18, one launch (start us, length us, event | category | flops | bytes accessed | tf_op | source)
XLA Modules:
  0.0 466.7 jit_solution(6522402630567856549)
XLA Ops:
  8.7 3.5 collective-permute-start.2
  12.1 2.4 collective-permute-start.3
  16.6 4.2 collective-permute-start
  27.6 5.1 %constant_dynamic-slice_fusion.2 = bf16[1,48,192,192]{3,2,1,0:T(8,128)(2,1)} fusion(bf16[2,48,192,192]{3,2,1,0:T(8,128)(2,1)} %param.3, s32[]{:T(128)S(6)} %select_n.74), kind=kLoop, calls=%fused_computation.107 | loop fusion | bytes 7077892 | tf_op jit(solution)/shard_map/jit(dynamic_index_in_dim)/dynamic_slice | solution.py:110
  33.7 7.0 %reshape.140 = bf16[24,73728]{1,0:T(8,128)(2,1)S(1)} reshape(bf16[1,48,192,192]{3,2,1,0:T(8,128)(2,1)} %constant_dynamic-slice_fusion.2) | data formatting | bytes 7077888 | tf_op jit(solution)/shard_map/reshape | solution.py:111
  40.8 2.2 dynamic-slice_bitcast_fusion
  44.6 4.7 %multiply_add_fusion = f32[30,3,96,96]{3,2,1,0:T(8,128)S(1)} fusion(f32[30,3,96,96]{3,2,1,0:T(8,128)S(1)} %pad_maximum_fusion.5), kind=kLoop, calls=%fused_computation.50 | loop fusion | flops 5806080 | bytes 6635520 | tf_op jit(solution)/shard_map/add | solution.py:27
  49.4 2.7 fusion.29
  52.1 3.3 fusion.36
  55.7 4.2 pad_maximum_fusion.4
  59.9 8.1 %reshape.141 = bf16[52,192,192]{2,1,0:T(8,128)(2,1)} reshape(bf16[26,73728]{1,0:T(8,128)(2,1)} %pad_maximum_fusion.4) | data formatting | bytes 7667712 | tf_op jit(solution)/shard_map/reshape | solution.py:113
  68.0 3.4 slice-done
  71.3 2.9 copy_convert_fusion
  74.2 4.1 copy-done
  78.3 5.1 %slice.199 = f32[48,192,192]{2,0,1:T(8,128)} slice(f32[50,192,192]{2,0,1:T(8,128)S(1)} %copy_convert_fusion), slice={[1:49], [0:192], [0:192]} | slice | bytes 14155776 | tf_op jit(solution)/shard_map/slice | solution.py:46
  83.4 28.5 %all-gather.3.cloned.1.call-done = bf16[104,3,96,96]{3,2,1,0:T(8,128)(2,1)} async-done(((bf16[26,3,96,96]{3,2,1,0:T(8,128)(2,1)}), bf16[104,3,96,96]{3,2,1,0:T(8,128)(2,1)}) %all-gather.3.cloned.1.call-update) | async-done | bytes 5750800 | tf_op jit(solution)/shard_map/all_gather | solution.py:106
  112.0 5.3 %select_reduce_fusion = bf16[26,3,96,96]{3,2,1,0:T(8,128)(2,1)S(1)} fusion(bf16[4,26,3,96,96]{4,3,2,1,0:T(8,128)(2,1)} %bitcast.51, pred[4]{0:T(512)(128)(4,1)S(1)} %copy-done.2), kind=kLoop, calls=%fused_computation.35 | loop fusion | flops 5031936 | bytes 7188484 | tf_op jit(solution)/shard_map/reduce_sum | solution.py:109
  118.5 12.9 %convolution_bitcast_fusion = f32[26,3,192,192]{3,2,1,0:T(8,128)S(1)} fusion(f32[26,3,96,192]{3,2,1,0:T(8,128)S(1)} %fusion.43, s32[192]{0:T(256)S(1)} %get-tuple-element.14, s32[192]{0:T(256)S(1)} %get-tuple-element.13), kind=kOutput, calls=%fused_computation.34 | convolution fusion | flops 3312543744 | bytes 17253888 | tf_op jit(solution)/shard_map/zcyX,Yy->zcYX/dot_general | solution.py:78
  131.5 43.9 %fusion = f32[48,3,192,192]{3,0,2,1:T(8,128)} fusion(f32[26,3,192,192]{3,2,1,0:T(8,128)S(1)} %convolution_bitcast_fusion, s32[48]{0:T(128)S(1)} %get-tuple-element.15, s32[48]{0:T(128)S(1)} %get-tuple-element.16), kind=kOutput, calls=%fused_computation | convolution fusion | flops 1656232064 | bytes 32735616 | tf_op jit(solution)/shard_map/zcYX,Zz->ZcYX/dot_general | solution.py:79
  175.4 39.4 %fusion.22 = f32[48,192,192]{2,0,1:T(8,128)} fusion(f32[48,192,192]{2,0,1:T(8,128)} %slice.199, f32[50,192,192]{2,0,1:T(8,128)} %copy-done, f32[48,3,192,192]{3,0,2,1:T(8,128)} %fusion, f32[]{:T(128)S(6)} %convert_element_type.30), kind=kLoop, calls=%fused_computation.27 | loop fusion | flops 23003136 | bytes 49545220 | tf_op jit(solution)/shard_map/mul | solution.py:114
  214.9 137.8 %all-reduce.10.cloned.1.call-done = f32[48,192,192]{2,0,1:T(8,128)} async-done(((f32[48,192,192]{2,0,1:T(8,128)}), f32[48,192,192]{2,0,1:T(8,128)}) %all-reduce.10.cloned.1.call-update) | async-done | bytes 7077904 | tf_op jit(solution)/shard_map/psum | solution.py:115
  352.6 4.7 %broadcast_multiply_fusion = f32[48,192,192]{2,0,1:T(8,128)S(1)} fusion(f32[48,192,192]{2,0,1:T(8,128)} %all-reduce.10.cloned.1.call-done), kind=kLoop, calls=%fused_computation.38 | loop fusion | flops 1769472 | bytes 14155776 | tf_op jit(solution)/shard_map/div | solution.py:116
  357.4 3.7 copy-done.1
  361.4 2.4 collective-permute-start.4
  363.9 3.4 collective-permute-start.5
  367.3 2.4 collective-permute-done.4
  371.9 32.0 %fusion.17 = f32[48,192,192]{2,0,1:T(8,128)} fusion(f32[48,192,192]{2,0,1:T(8,128)} %copy-done.1, f32[1,192,192]{2,0,1:T(1,128)S(1)} %collective-permute-done.5, f32[1,192,192]{2,0,1:T(1,128)S(1)} %collective-permute-done.4, f32[48,192,192]{2,0,1:T(8,128)} %all-reduce.10.cloned.1.call-done), kind=kLoop, calls=%fused_computation.20 | loop fusion | flops 19464192 | bytes 21528576 | tf_op jit(solution)/shard_map/add | solution.py:67
  406.0 2.4 collective-permute-start.6
  408.5 3.4 collective-permute-start.7
  413.6 2.5 collective-permute-done.7
  416.0 30.7 %fusion.9 = f32[48,192,192]{2,0,1:T(8,128)} fusion(f32[48,192,192]{2,0,1:T(8,128)} %fusion.17, f32[1,192,192]{2,0,1:T(1,128)S(1)} %collective-permute-done.7, f32[1,192,192]{2,0,1:T(1,128)S(1)} %collective-permute-done.6), kind=kLoop, calls=%fused_computation.10 | loop fusion | flops 19464192 | bytes 14450688 | tf_op jit(solution)/shard_map/add | solution.py:67
  446.7 12.9 %copy.9 = f32[48,192,192]{2,1,0:T(8,128)} copy(f32[48,192,192]{2,0,1:T(8,128)} %fusion.9) | data formatting | bytes 14155776 | tf_op jit(solution)/shard_map/add | solution.py:67
  (31 shorter events, 18.8 us)
Async XLA Ops:
  6.5 105.4 %all-gather.3.cloned.1.call-start = ((), (), s32[]{:S(2)}) async-start(), calls=%async_computation.1 | async-start | bytes 9584640 | tf_op jit(solution)/shard_map/all_gather | solution.py:106
  8.7 34.4 %collective-permute-start.2 = (f32[3,3,96,96]{3,2,1,0:T(8,128)}, f32[3,3,96,96]{3,2,1,0:T(8,128)}, u32[]{:S(2)}, u32[]{:S(2)}) collective-permute-start(f32[3,3,96,96]{3,2,1,0:T(8,128)} %get-tuple-element.11), channel_id=1, source_target_pairs={{0,1},{1,2},{2,3},{4,5},{5,6},{6,7},{8,9},{9,10},{10,11},{12,13},{... | collective-permute-start | bytes 995336 | tf_op jit(solution)/shard_map/ppermute | solution.py:16
  12.1 30.9 %collective-permute-start.3 = (f32[3,3,96,96]{3,2,1,0:T(8,128)}, f32[3,3,96,96]{3,2,1,0:T(8,128)}, u32[]{:S(2)}, u32[]{:S(2)}) collective-permute-start(f32[3,3,96,96]{3,2,1,0:T(8,128)} %get-tuple-element.12), channel_id=1, source_target_pairs={{1,0},{2,1},{3,2},{5,4},{6,5},{7,6},{9,8},{10,9},{11,10},{13,12},{... | collective-permute-start | bytes 995336 | tf_op jit(solution)/shard_map/ppermute | solution.py:17
  16.6 39.1 %collective-permute-start = (bf16[1,73728]{1,0:T(2,128)(2,1)}, bf16[1,73728]{1,0:T(2,128)(2,1)}, u32[]{:S(2)}, u32[]{:S(2)}) collective-permute-start(bf16[1,73728]{1,0:T(2,128)(2,1)} %slice.151), channel_id=1, source_target_pairs={{0,1},{1,2},{2,3},{4,5},{5,6},{6,7},{8,9},{9,10},{10,11},{12,13},{... | collective-permute-start | bytes 442376 | tf_op jit(solution)/shard_map/ppermute | solution.py:16
  21.8 33.8 %collective-permute-start.1 = (bf16[1,73728]{1,0:T(2,128)(2,1)}, bf16[1,73728]{1,0:T(2,128)(2,1)}, u32[]{:S(2)}, u32[]{:S(2)}) collective-permute-start(bf16[1,73728]{1,0:T(2,128)(2,1)} %slice.153), channel_id=1, source_target_pairs={{1,0},{2,1},{3,2},{5,4},{6,5},{7,6},{9,8},{10,9},{11,10},{13,12},{... | collective-permute-start | bytes 442376 | tf_op jit(solution)/shard_map/ppermute | solution.py:17
  44.6 7.5 %copy-start.3 = (pred[26]{0:T(512)(128)(4,1)S(1)}, pred[26]{0:T(512)(128)(4,1)}, u32[]{:S(2)}) copy-start(pred[26]{0:T(512)(128)(4,1)} %compare_and_fusion) | copy-start | bytes 82
  55.4 297.2 %all-reduce.10.cloned.1.call-start = ((), (), s32[]{:S(2)}) async-start(), calls=%async_computation | async-start | bytes 18874368 | tf_op jit(solution)/shard_map/psum | solution.py:115
  68.0 3.4 slice-start
  74.2 4.1 copy-start
  78.3 33.7 %copy-start.2 = (pred[4]{0:T(512)(128)(4,1)S(1)}, pred[4]{0:T(512)(128)(4,1)}, u32[]{:S(2)}) copy-start(pred[4]{0:T(512)(128)(4,1)} %iota_compare_fusion.8) | copy-start | bytes 16
  357.4 3.7 copy-start.1
  361.4 8.3 %collective-permute-start.4 = (f32[1,192,192]{2,0,1:T(1,128)S(1)}, f32[1,192,192]{2,0,1:T(1,128)S(1)}, u32[]{:S(2)}, u32[]{:S(2)}) collective-permute-start(f32[1,192,192]{2,0,1:T(1,128)S(1)} %get-tuple-element.7), channel_id=1, source_target_pairs={{1,0},{2,1},{3,2},{5,4},{6,5},{7,6},{9,8},{10,9},{11,10},{13,12},{... | collective-permute-start | bytes 442376 | tf_op jit(solution)/shard_map/ppermute | solution.py:17
  363.9 8.0 %collective-permute-start.5 = (f32[1,192,192]{2,0,1:T(1,128)S(1)}, f32[1,192,192]{2,0,1:T(1,128)S(1)}, u32[]{:S(2)}, u32[]{:S(2)}) collective-permute-start(f32[1,192,192]{2,0,1:T(1,128)S(1)} %get-tuple-element.8), channel_id=1, source_target_pairs={{0,1},{1,2},{2,3},{4,5},{5,6},{6,7},{8,9},{9,10},{10,11},{12,13},{... | collective-permute-start | bytes 442376 | tf_op jit(solution)/shard_map/ppermute | solution.py:16
  406.0 7.6 %collective-permute-start.6 = (f32[1,192,192]{2,0,1:T(1,128)S(1)}, f32[1,192,192]{2,0,1:T(1,128)S(1)}, u32[]{:S(2)}, u32[]{:S(2)}) collective-permute-start(f32[1,192,192]{2,0,1:T(1,128)S(1)} %get-tuple-element.5), channel_id=1, source_target_pairs={{1,0},{2,1},{3,2},{5,4},{6,5},{7,6},{9,8},{10,9},{11,10},{13,12},{... | collective-permute-start | bytes 442376 | tf_op jit(solution)/shard_map/ppermute | solution.py:17
  408.5 7.6 %collective-permute-start.7 = (f32[1,192,192]{2,0,1:T(1,128)S(1)}, f32[1,192,192]{2,0,1:T(1,128)S(1)}, u32[]{:S(2)}, u32[]{:S(2)}) collective-permute-start(f32[1,192,192]{2,0,1:T(1,128)S(1)} %get-tuple-element.6), channel_id=1, source_target_pairs={{0,1},{1,2},{2,3},{4,5},{5,6},{6,7},{8,9},{9,10},{10,11},{12,13},{... | collective-permute-start | bytes 442376 | tf_op jit(solution)/shard_map/ppermute | solution.py:16
Sparse Core Ops, SparseCore 0:
  55.6 56.3 all-gather.2
  215.0 137.6 all-reduce.9
where the time goes:
time: 474 us; the launch traced here: 467 us
  waiting for transfers between devices  175 us (37%)
  other arithmetic  133 us (28%)
  local copies, waits for them, and re-layouts  60.4 us (13%)
  matrix products  58.1 us (12%)
  starting transfers between devices  23.9 us (5%)
  between operations  16.4 us (3%)
    psum x1, waiting for transfers between devices, shards(): summed = lax.psum(total, ('level', 'subj'))  138 us
    add x2, other arithmetic, relax(): return center + 0.15 * (neighbours - 6.0 * center)  62.7 us
    dot_general x1, matrix products, upsample(): return jnp.einsum('zcYX,Zz->ZcYX', section_y, table_z, precision=highest)  43.9 us
    mul x1, other arithmetic, shards(): weight * warp_slab(image_ext.astype(jnp.float32), upsample(arrived, table...  39.4 us
    all_gather x1, waiting for transfers between devices, shards(): piece = lax.all_gather(field[None], 'subj', axis=0, tiled=True)  28.5 us
    ppermute x4, starting transfers between devices, with_halo(): before = lax.ppermute(last, axis, up)  14.5 us
    dot_general x1, matrix products, upsample(): jnp.einsum('zcyX,Yy->zcYX', section_x, table_xy, precision=highest)  12.9 us
    add x1, local copies, waits for them, and re-layouts, relax(): return center + 0.15 * (neighbours - 6.0 * center)  12.9 us
  transfers between devices with their start and end apart: 10, of which 6 were waited for; matrix products, arithmetic and copies ran while one was open for 11% of the time, Pallas kernels for 0%

commit v1 on v0

v1 whole, which is shorter than its diff:
```python
import jax
import jax.numpy as jnp
from jax import lax
from jax.experimental import pallas as pl
from jax.experimental.pallas import tpu as pltpu
from jax.sharding import PartitionSpec as P

SWEEPS = 2


def with_halo(array, sides, width):
    for axis, dim in sides:
        size, length = (lax.axis_size(axis), array.shape[dim])
        up = [(i, (i + 1) % size) for i in range(size - 1)]
        down = [(j, i) for i, j in up]
        last = lax.slice_in_dim(array, length - width, length, axis=dim)
        leading = lax.slice_in_dim(array, 0, width, axis=dim)
        before = lax.ppermute(last, axis, up)
        after = lax.ppermute(leading, axis, down)
        array = jnp.concatenate([before, array, after], axis=dim)
    return array


def band(padded, count, axis):

    def take(offset):
        return lax.slice_in_dim(padded, offset, offset + count, axis=axis)

    return (take(0) + take(4)) * 0.0625 + (take(1) + take(3)) * 0.25 + take(2) * 0.375


def blur_plane(field, axis):
    widths = [(2, 2) if dimension == axis else (0, 0) for dimension in range(field.ndim)]
    return band(jnp.pad(field, widths), field.shape[axis], axis)


def upsample_table(finest, coarse, offset):
    rows_fine = jnp.arange(finest, dtype=jnp.int32)[:, None]
    columns = jnp.arange(coarse, dtype=jnp.int32)[None, :]
    nearest = rows_fine // 2 + offset
    farther = nearest + 2 * (rows_fine % 2) - 1
    return 0.75 * (columns == nearest).astype(jnp.float32) + 0.25 * (columns == farther).astype(
        jnp.float32
    )


def halo_rows(first, last, axis):
    size = lax.axis_size(axis)
    up = [(i, (i + 1) % size) for i in range(size - 1)]
    down = [(j, i) for i, j in up]
    return lax.ppermute(last, axis, up), lax.ppermute(first, axis, down)


def slope_table(finest):
    rows = jnp.arange(finest, dtype=jnp.int32)[:, None]
    columns = jnp.arange(finest, dtype=jnp.int32)[None, :]
    ahead = (columns == rows + 1).astype(jnp.float32)
    behind = (columns == rows - 1).astype(jnp.float32)
    return ((ahead - behind) * 0.5).astype(jnp.bfloat16)


LANES = 128


def pack_coarse(field):
    coarse = field.shape[-1]
    rest = LANES - coarse
    kept = coarse * coarse // LANES
    tail = field[..., kept:, :]
    pieces = [tail[..., i : i + rest] for i in range(0, coarse, rest)]
    return jnp.concatenate([field[..., :kept, :], jnp.concatenate(pieces, axis=-2)], axis=-1)


def warp_kernel(
    sel, velocity, pair, below, above, before, after, up_x, up_y, slope_x, slope_y, out, fine
):
    step = pl.program_id(0)
    last = pl.num_programs(0) - 1
    for c in range(3):
        packed = velocity[0, 0, c]
        parts = [
            jnp.dot(packed, up_x[i], preferred_element_type=jnp.float32)
            for i in range(up_x.shape[0])
        ]
        size = packed.shape[0] // (len(parts) - 1)
        tail = parts[1][:size]
        for i in range(2, len(parts)):
            tail = tail + parts[i][(i - 1) * size : i * size]
        wide = jnp.concatenate([parts[0], tail], axis=0)
        high = wide.astype(jnp.bfloat16)
        low = (wide - high.astype(jnp.float32)).astype(jnp.bfloat16)
        both = jnp.concatenate([high, low], axis=0)
        fine[lax.rem(step, 3), c] = jnp.dot(up_y[...], both, preferred_element_type=jnp.float32)

    @pl.when(step >= 2)
    def _():
        finest = pair.shape[2]
        half = finest // 2
        rest = finest - LANES
        chunk = finest // 4
        scale = sel[2].astype(jnp.float32) * (1.0 / sel[3].astype(jnp.float32))
        middle = lax.rem(step + 2, 3)
        prior_is_halo = step == 2
        next_is_halo = step == last
        for z in range(2):
            outer = lax.rem(step + 1, 3) if z == 0 else lax.rem(step, 3)
            for r in range(0, finest, chunk):
                rows = pl.ds(r, chunk)
                image = pair[0, z, rows, :]
                dx = jnp.dot(image, slope_x[...], preferred_element_type=jnp.float32)
                dy = jnp.dot(
                    slope_y[rows, :], pair[0, z], preferred_element_type=jnp.float32
                )
                if z == 0:
                    back = jnp.where(
                        prior_is_halo,
                        before[0, rows, :].astype(jnp.float32),
                        below[0, 0, rows, :].astype(jnp.float32),
                    )
                    ahead = pair[0, 1, rows, :].astype(jnp.float32)
                else:
                    back = pair[0, 0, rows, :].astype(jnp.float32)
                    ahead = jnp.where(
                        next_is_halo,
                        after[0, rows, :].astype(jnp.float32),
                        above[0, 0, rows, :].astype(jnp.float32),
                    )
                dz = (ahead - back) * 0.5
                near = (
                    fine[middle, 0, rows, :] * dx
                    + fine[middle, 1, rows, :] * dy
                    + fine[middle, 2, rows, :] * dz
                )
                far = (
                    fine[outer, 0, rows, :] * dx
                    + fine[outer, 1, rows, :] * dy
                    + fine[outer, 2, rows, :] * dz
                )
                value = scale * (image.astype(jnp.float32) - (0.75 * near + 0.25 * far))
                out[z, rows, :] = value[:, :LANES]
                side = rest * (r // half)
                out[z, pl.ds(finest + r % half, chunk), side : side + rest] = value[:, LANES:]


def warp(sel, gathered, images, before, after, interpret=False):
    finest = images.shape[2]
    slab_ext, kept = gathered.shape[1], gathered.shape[3]
    coarse = finest // 2
    rest = LANES - coarse
    fine_slab = images.shape[1]
    table = upsample_table(finest, coarse, 0).astype(jnp.bfloat16)
    columns = table.T
    up_x = [jnp.pad(columns, ((0, rest), (0, 0)))]
    for i in range(0, coarse, rest):
        up_x.append(jnp.pad(columns[i : i + rest], ((coarse, 0), (0, 0))))
    up_x = jnp.stack(up_x)
    slope = slope_table(finest)
    whole = lambda j, s: (0, 0)
    edge = lambda j, s: (0, 0, 0)
    lag = lambda j: jnp.maximum(j - 2, 0)
    plane = (1, 1, finest, finest)
    grid_spec = pltpu.PrefetchScalarGridSpec(
        num_scalar_prefetch=1,
        grid=(slab_ext,),
        in_specs=[
            pl.BlockSpec((1, 1, 3, kept, LANES), lambda j, s: (s[1], j, 0, 0, 0)),
            pl.BlockSpec((1, 2, finest, finest), lambda j, s: (s[0], lag(j), 0, 0)),
            pl.BlockSpec(plane, lambda j, s: (s[0], jnp.maximum(2 * lag(j) - 1, 0), 0, 0)),
            pl.BlockSpec(
                plane, lambda j, s: (s[0], jnp.minimum(2 * lag(j) + 2, fine_slab - 1), 0, 0)
            ),
            pl.BlockSpec((1, finest, finest), edge),
            pl.BlockSpec((1, finest, finest), edge),
            pl.BlockSpec(up_x.shape, edge),
            pl.BlockSpec((finest, 2 * coarse), whole),
            pl.BlockSpec((finest, finest), whole),
            pl.BlockSpec((finest, finest), whole),
        ],
        out_specs=pl.BlockSpec(
            (2, finest + finest // 2, LANES), lambda j, s: (lag(j), 0, 0)
        ),
        scratch_shapes=[pltpu.VMEM((3, 3, finest, finest), jnp.float32)],
    )
    return pl.pallas_call(
        warp_kernel,
        grid_spec=grid_spec,
        out_shape=jax.ShapeDtypeStruct((fine_slab, finest + finest // 2, LANES), jnp.float32),
        compiler_params=pltpu.CompilerParams(dimension_semantics=("arbitrary",)),
        interpret=interpret,
    )(
        sel,
        gathered,
        images,
        images,
        images,
        before,
        after,
        up_x,
        jnp.concatenate([table, table], axis=1),
        slope.T,
        slope,
    )


MARGIN = 8


def relax_row(ref, slot, behind, ahead, r, chunk):
    rows = pl.ds(MARGIN + r, chunk)
    center = ref[slot, rows, :]
    width = center.shape[1]
    neighbours = (
        ref[behind, rows, :]
        + ref[ahead, rows, :]
        + ref[slot, pl.ds(MARGIN + r - 1, chunk), :]
        + ref[slot, pl.ds(MARGIN + r + 1, chunk), :]
        + pltpu.roll(center, 1, 1)
        + pltpu.roll(center, width - 1, 1)
    )
    return center + 0.15 * (neighbours - 6.0 * center)


def sweep_kernel(sel, mean, before, after, out, first, second):
    step = pl.program_id(0)
    last = pl.num_programs(0) - 1
    finest = out.shape[1]
    half = finest // 2
    rest = finest - LANES
    chunk = finest // 3
    base = 2 * lax.rem(step, 2)
    other = 2 - base

    def enter(ref):
        for z in range(2):
            slot = base + z
            first[slot, pl.ds(MARGIN, finest), 0:LANES] = ref[z, 0:finest, :]
            side = ref[z, finest : finest + half, :]
            first[slot, pl.ds(MARGIN, half), LANES:finest] = side[:, :rest]
            turned = pltpu.roll(side, LANES - rest, 1)
            first[slot, pl.ds(MARGIN + half, half), LANES:finest] = turned[:, :rest]

    @pl.when(step == 0)
    def _():
        first[...] = jnp.zeros_like(first)
        second[...] = jnp.zeros_like(second)
        enter(before)

    @pl.when((step > 0) & (step < last))
    def _():
        enter(mean)

    @pl.when(step == last)
    def _():
        enter(after)

    @pl.when(step >= 1)
    def _():
        keep_low = jnp.where((step == 1) & (sel[0] == 0), 0.0, 1.0)
        keep_high = jnp.where((step == last) & (sel[0] == sel[1]), 0.0, 1.0)
        places = ((other + 1, other, base, keep_low), (base, other + 1, base + 1, keep_high))
        for slot, behind, ahead, keep in places:
            for r in range(0, finest, chunk):
                value = relax_row(first, slot, behind, ahead, r, chunk) * keep
                second[slot, pl.ds(MARGIN + r, chunk), 0:finest] = value[:, :finest]

    @pl.when(step >= 2)
    def _():
        places = ((other, base + 1, other + 1), (other + 1, other, base))
        for z, (slot, behind, ahead) in enumerate(places):
            for r in range(0, finest, chunk):
                value = relax_row(second, slot, behind, ahead, r, chunk)
                out[z, pl.ds(r, chunk), :] = value[:, :finest]


def sweeps(sel, mean, before, after, finest, interpret=False):
    fine_slab = mean.shape[0]
    blocks = fine_slab // 2
    block = (2,) + mean.shape[1:]
    width = -(-(finest + 1) // LANES) * LANES
    ring = pltpu.VMEM((4, finest + 2 * MARGIN, width), jnp.float32)
    grid_spec = pltpu.PrefetchScalarGridSpec(
        num_scalar_prefetch=1,
        grid=(blocks + 2,),
        in_specs=[
            pl.BlockSpec(block, lambda j, s: (jnp.clip(j - 1, 0, blocks - 1), 0, 0)),
            pl.BlockSpec(block, lambda j, s: (0, 0, 0)),
            pl.BlockSpec(block, lambda j, s: (0, 0, 0)),
        ],
        out_specs=pl.BlockSpec(
            (2, finest, finest), lambda j, s: (jnp.maximum(j - 2, 0), 0, 0)
        ),
        scratch_shapes=[ring, ring],
    )
    return pl.pallas_call(
        sweep_kernel,
        grid_spec=grid_spec,
        out_shape=jax.ShapeDtypeStruct((fine_slab, finest, finest), jnp.float32),
        compiler_params=pltpu.CompilerParams(dimension_semantics=("arbitrary",)),
        interpret=interpret,
    )(sel, mean, before, after)


def shards(images, momenta, assign):
    count = momenta.shape[0]
    slab = momenta.shape[1]
    coarse = momenta.shape[3]
    finest = images.shape[2]
    fine_slab = images.shape[1]
    level_index = lax.axis_index("level")
    group_index = lax.axis_index("subj")
    zone_index = lax.axis_index("gz")
    rim_width = 3
    ticker = 0 + level_index
    weight = (ticker < count).astype(jnp.int32)
    ticker = jnp.minimum(ticker, count - 1)
    moment = lax.dynamic_index_in_dim(momenta, ticker, 0, keepdims=False)
    extended = with_halo(moment, (("gz", 0),), rim_width)
    smooth = blur_plane(blur_plane(extended, 3), 2)
    field = band(smooth, extended.shape[0] - 4, 0)
    global_z = zone_index * slab - 1 + jnp.arange(field.shape[0], dtype=jnp.int32)
    inside = (global_z >= 0) & (global_z < slab * lax.axis_size("gz"))
    field = jnp.where(inside[:, None, None, None], field, 0.0)
    field = pack_coarse(field.astype(jnp.bfloat16))
    source = assign[group_index * count + ticker] // count
    piece = lax.all_gather(field[None], "subj", axis=0, tiled=True)
    rows = lax.dynamic_slice_in_dim(images, ticker, 1, 0)
    image_before, image_after = halo_rows(rows[0, :1], rows[0, fine_slab - 1 :], "gz")
    subjects = jnp.int32(lax.axis_size("subj") * count)
    sel = jnp.stack([ticker, source, weight, subjects]).astype(jnp.int32)
    total = warp(sel, piece, images, image_before, image_after)
    mean = lax.psum(total, ("level", "subj"))
    mean_before, mean_after = halo_rows(mean[:2], mean[fine_slab - 2 :], "gz")
    zones = jnp.stack([zone_index, lax.axis_size("gz") - 1]).astype(jnp.int32)
    return sweeps(zones, mean, mean_before, mean_after, finest)


def solution(mesh):
    return jax.shard_map(
        shards,
        mesh=mesh,
        in_specs=(P("subj", "gz", None, None), P("subj", "gz", None, None, None), P()),
        out_specs=P("gz", None, None),
        check_vma=False,
    )
```

time: 474 us -> 279 us (0.59); the launches traced: 467 us -> 278 us
  other arithmetic: 133 us -> 15.8 us
  Pallas kernels: 0 us -> 63 us
  matrix products: 58.1 us -> 0 us
  local copies, waits for them, and re-layouts: 60.4 us -> 7.36 us
  waiting for transfers between devices: 175 us -> 158 us
  starting transfers between devices: 23.9 us -> 17.6 us
    pallas_call x0 -> x2, Pallas kernels: none -> 63 us  [the longest x1 38 us: warp(): pl.pallas_call(warp_kernel, grid_spec=grid_spec, out_shape=jax.ShapeDtype...]
    add x2 -> x0, other arithmetic: 62.7 us -> none  [relax(): return center + 0.15 * (neighbours - 6.0 * center)]
    dot_general x3 -> x0, matrix products: 58.1 us -> none  [the longest x1 43.9 us: upsample(): return jnp.einsum('zcYX,Zz->ZcYX', section_y, table_z, precision=highest)]
    mul x1 -> x0, other arithmetic: 39.4 us -> none  [shards(): weight * warp_slab(image_ext.astype(jnp.float32), upsample(arrived, table...]
    psum x1, waiting for transfers between devices: 138 us -> 113 us  [shards(): mean = lax.psum(total, ('level', 'subj'))]
    reshape x2 -> x0, local copies, waits for them, and re-layouts: 15.1 us -> none  [the longest x1 8.1 us: shards(): image_ext = extended.reshape(2 * slab + 4, finest, finest)[1:-1]]
    add x1 -> x0, local copies, waits for them, and re-layouts: 12.9 us -> none  [relax(): return center + 0.15 * (neighbours - 6.0 * center)]
    ppermute x0 -> x4, starting transfers between devices: none -> 11.7 us  [halo_rows(): return (lax.ppermute(last, axis, up), lax.ppermute(first, axis, down))]
  transfers between devices with their start and end apart: 10 -> 8, of which waited for: 6 -> 6; matrix products, arithmetic and copies ran while one was open for 11% -> 3% of each run, Pallas kernels for 0% -> 0%
where the time goes in v1:
time: 279 us; the launch traced here: 278 us
  waiting for transfers between devices  158 us (57%)
  Pallas kernels  63 us (23%)
  starting transfers between devices  17.6 us (6%)
  between operations  16.4 us (6%)
  other arithmetic  15.8 us (6%)
  local copies, waits for them, and re-layouts  7.36 us (3%)
    psum x1, waiting for transfers between devices, shards(): mean = lax.psum(total, ('level', 'subj'))  113 us
    pallas_call x1, Pallas kernels, warp(): pl.pallas_call(warp_kernel, grid_spec=grid_spec, out_shape=jax.ShapeDtype...  38 us
    all_gather x1, waiting for transfers between devices, shards(): piece = lax.all_gather(field[None], 'subj', axis=0, tiled=True)  30 us
    pallas_call x1, Pallas kernels, sweeps(): pl.pallas_call(sweep_kernel, grid_spec=grid_spec, out_shape=jax.ShapeDtyp...  25 us
    ppermute x4, starting transfers between devices, halo_rows(): return (lax.ppermute(last, axis, up), lax.ppermute(first, axis, down))  11.7 us
    add x2, other arithmetic, band(): (take(0) + take(4)) * 0.0625 + (take(1) + take(3)) * 0.25 + take(2) * 0.375  7.44 us
    ppermute x4, waiting for transfers between devices, halo_rows(): return (lax.ppermute(last, axis, up), lax.ppermute(first, axis, down))  6.01 us
    ppermute x1, waiting for transfers between devices, with_halo(): before = lax.ppermute(last, axis, up)  5.68 us
  transfers between devices with their start and end apart: 8, of which 6 were waited for; matrix products, arithmetic and copies ran while one was open for 3% of the time, Pallas kernels for 0%

profile of v1, /device:TPU:18, one launch (start us, length us, event | category | flops | bytes accessed | tf_op | source)
XLA Modules:
  0.0 277.8 jit_solution(7556803504424575824)
XLA Ops:
  6.5 1.2 dynamic-slice_bitcast_fusion.2
  7.7 3.5 %collective-permute-start = (f32[3,3,96,96]{3,2,1,0:T(8,128)S(1)}, f32[3,3,96,96]{3,2,1,0:T(8,128)S(1)}, u32[]{:S(2)}, u32[]{:S(2)}) collective-permute-start(f32[3,3,96,96]{3,2,1,0:T(8,128)S(1)} %get-tuple-element.9), channel_id=1, source_target_pairs={{0,1},{1,2},{2,3},{4,5},{5,6},{6,7},{8,9},{9,10},{10,11},{12,13},{... | collective-permute-start | bytes 995336 | tf_op jit(solution)/shard_map/ppermute | solution.py:18
  11.2 2.4 collective-permute-start.1
  13.6 2.2 dynamic-slice_bitcast_fusion
  15.9 5.7 %collective-permute-done = f32[3,3,96,96]{3,2,1,0:T(8,128)S(1)} collective-permute-done((f32[3,3,96,96]{3,2,1,0:T(8,128)S(1)}, f32[3,3,96,96]{3,2,1,0:T(8,128)S(1)}, u32[]{:S(2)}, u32[]{:S(2)}) %collective-permute-start) | collective-permute-done | bytes 331808 | tf_op jit(solution)/shard_map/ppermute | solution.py:18
  21.5 3.2 %collective-permute-done.1 = f32[3,3,96,96]{3,2,1,0:T(8,128)S(1)} collective-permute-done((f32[3,3,96,96]{3,2,1,0:T(8,128)S(1)}, f32[3,3,96,96]{3,2,1,0:T(8,128)S(1)}, u32[]{:S(2)}, u32[]{:S(2)}) %collective-permute-start.1) | collective-permute-done | bytes 331808 | tf_op jit(solution)/shard_map/ppermute | solution.py:19
  24.8 0.4 pad_maximum_fusion
  25.2 4.7 %multiply_add_fusion = f32[30,3,96,96]{3,2,1,0:T(8,128)S(1)} fusion(f32[30,3,96,96]{3,2,1,0:T(8,128)S(1)} %pad_maximum_fusion), kind=kLoop, calls=%fused_computation.11 | loop fusion | flops 5806080 | bytes 6635520 | tf_op jit(solution)/shard_map/add | solution.py:29
  29.9 2.7 fusion.3
  32.6 2.4 fusion.10
  35.1 0.3 fusion.20
  35.5 1.9 maximum_maximum_fusion
  37.4 1.0 dynamic-slice_bitcast_fusion.3
  38.4 2.4 collective-permute-start.3
  40.8 3.5 %collective-permute-start.2 = (bf16[1,192,192]{2,1,0:T(8,128)(2,1)S(1)}, bf16[1,192,192]{2,1,0:T(8,128)(2,1)S(1)}, u32[]{:S(2)}, u32[]{:S(2)}) collective-permute-start(bf16[1,192,192]{2,1,0:T(8,128)(2,1)S(1)} %get-tuple-element.6), channel_id=1, source_target_pairs={{0,1},{1,2},{2,3},{4,5},{5,6},{6,7},{8,9},{9,10},{10,11},{12,13},{... | collective-permute-start | bytes 221192 | tf_op jit(solution)/shard_map/ppermute | solution.py:51
  44.3 0.7 dynamic_slice.10
  47.8 0.1 add_convert_fusion
  48.0 0.7 pad_maximum_fusion.2.up_y
  48.7 0.7 pad_maximum_fusion.1.up_x
  49.5 0.8 multiply_convert_fusion
  50.3 0.6 pad_add_fusion.1.sel
  50.9 30.0 %all-gather.3.cloned.1.call-done = bf16[104,3,72,128]{3,2,1,0:T(8,128)(2,1)} async-done(((bf16[26,3,72,128]{3,2,1,0:T(8,128)(2,1)}), bf16[104,3,72,128]{3,2,1,0:T(8,128)(2,1)}) %all-gather.3.cloned.1.call-update) | async-done | bytes 5750800 | tf_op jit(solution)/shard_map/all_gather | solution.py:325
  80.9 38.0 %shard_map.37 = f32[48,288,128]{2,1,0:T(8,128)} custom-call(s32[4]{0:T(128)} %pad_add_fusion.1.sel, bf16[4,26,3,72,128]{4,3,2,1,0:T(8,128)(2,1)} %bitcast.24, bf16[2,48,192,192]{3,2,1,0:T(8,128)(2,1)} %above.1, bf16[2,48,192,192]{3,2,1,0:T(8,128)(2,1)} %above.1, bf16[2,48,192,192]{3,2,1,0:T(8,128)(2,1)} %above.1, bf16[1,192,192]{2,1,0:T(8,128)(2,1)} %copy-done.3, ...), custom_call_target="tpu_custom_call" | custom-call | tf_op jit(solution)/shard_map/pallas_call | solution.py:184
  118.9 112.7 %all-reduce.8.cloned.1.call-done.mean = f32[48,288,128]{2,1,0:T(8,128)} async-done(((f32[48,288,128]{2,1,0:T(8,128)}), f32[48,288,128]{2,1,0:T(8,128)}) %all-reduce.8.cloned.1.call-update) | async-done | bytes 7077904 | tf_op jit(solution)/shard_map/psum | solution.py:331
  231.6 1.1 fusion.19
  232.7 2.4 collective-permute-start.5
  235.2 3.4 %collective-permute-start.4 = (f32[2,288,128]{2,1,0:T(8,128)S(1)}, f32[2,288,128]{2,1,0:T(8,128)S(1)}, u32[]{:S(2)}, u32[]{:S(2)}) collective-permute-start(f32[2,288,128]{2,1,0:T(8,128)S(1)} %get-tuple-element.8), channel_id=1, source_target_pairs={{0,1},{1,2},{2,3},{4,5},{5,6},{6,7},{8,9},{9,10},{10,11},{12,13},{... | collective-permute-start | bytes 884744 | tf_op jit(solution)/shard_map/ppermute | solution.py:51
  238.6 0.7 pad_add_fusion.sel
  239.2 3.8 %collective-permute-done.5.after = f32[2,288,128]{2,1,0:T(8,128)S(1)} collective-permute-done((f32[2,288,128]{2,1,0:T(8,128)S(1)}, f32[2,288,128]{2,1,0:T(8,128)S(1)}, u32[]{:S(2)}, u32[]{:S(2)}) %collective-permute-start.5) | collective-permute-done | bytes 294944 | tf_op jit(solution)/shard_map/ppermute | solution.py:51
  243.1 2.2 collective-permute-done.4.before
  245.3 0.7 copy-done.1
  246.0 25.0 %shard_map.38 = f32[48,192,192]{2,1,0:T(8,128)} custom-call(s32[2]{0:T(128)} %pad_add_fusion.sel, f32[48,288,128]{2,1,0:T(8,128)} %all-reduce.8.cloned.1.call-done.mean, f32[2,288,128]{2,1,0:T(8,128)} %copy-done.1, f32[2,288,128]{2,1,0:T(8,128)} %copy-done), custom_call_target="tpu_custom_call" | custom-call | tf_op jit(solution)/shard_map/pallas_call | solution.py:294
  (25 shorter events, 0.3 us)
Async XLA Ops:
  6.5 74.3 %all-gather.3.cloned.1.call-start = ((), (), s32[]{:S(2)}) async-start(), calls=%async_computation.1 | async-start | bytes 7188480 | tf_op jit(solution)/shard_map/all_gather | solution.py:325
  7.7 13.8 %collective-permute-start = (f32[3,3,96,96]{3,2,1,0:T(8,128)S(1)}, f32[3,3,96,96]{3,2,1,0:T(8,128)S(1)}, u32[]{:S(2)}, u32[]{:S(2)}) collective-permute-start(f32[3,3,96,96]{3,2,1,0:T(8,128)S(1)} %get-tuple-element.9), channel_id=1, source_target_pairs={{0,1},{1,2},{2,3},{4,5},{5,6},{6,7},{8,9},{9,10},{10,11},{12,13},{... | collective-permute-start | bytes 995336 | tf_op jit(solution)/shard_map/ppermute | solution.py:18
  11.2 13.5 %collective-permute-start.1 = (f32[3,3,96,96]{3,2,1,0:T(8,128)S(1)}, f32[3,3,96,96]{3,2,1,0:T(8,128)S(1)}, u32[]{:S(2)}, u32[]{:S(2)}) collective-permute-start(f32[3,3,96,96]{3,2,1,0:T(8,128)S(1)} %get-tuple-element.10), channel_id=1, source_target_pairs={{1,0},{2,1},{3,2},{5,4},{6,5},{7,6},{9,8},{10,9},{11,10},{13,12},{... | collective-permute-start | bytes 995336 | tf_op jit(solution)/shard_map/ppermute | solution.py:19
  35.1 9.1 %copy-start.4 = (s32[8]{0:T(128)S(1)}, s32[8]{0:T(128)}, u32[]{:S(2)}) copy-start(s32[8]{0:T(128)} %param.5) | copy-start | bytes 100
  37.4 194.3 %all-reduce.8.cloned.1.call-start = ((), (), s32[]{:S(2)}) async-start(), calls=%async_computation | async-start | bytes 14155776 | tf_op jit(solution)/shard_map/psum | solution.py:331
  38.4 12.5 %collective-permute-start.3 = (bf16[1,192,192]{2,1,0:T(8,128)(2,1)S(1)}, bf16[1,192,192]{2,1,0:T(8,128)(2,1)S(1)}, u32[]{:S(2)}, u32[]{:S(2)}) collective-permute-start(bf16[1,192,192]{2,1,0:T(8,128)(2,1)S(1)} %get-tuple-element.5), channel_id=1, source_target_pairs={{1,0},{2,1},{3,2},{5,4},{6,5},{7,6},{9,8},{10,9},{11,10},{13,12},{... | collective-permute-start | bytes 221192 | tf_op jit(solution)/shard_map/ppermute | solution.py:51
  40.8 10.1 %collective-permute-start.2 = (bf16[1,192,192]{2,1,0:T(8,128)(2,1)S(1)}, bf16[1,192,192]{2,1,0:T(8,128)(2,1)S(1)}, u32[]{:S(2)}, u32[]{:S(2)}) collective-permute-start(bf16[1,192,192]{2,1,0:T(8,128)(2,1)S(1)} %get-tuple-element.6), channel_id=1, source_target_pairs={{0,1},{1,2},{2,3},{4,5},{5,6},{6,7},{8,9},{9,10},{10,11},{12,13},{... | collective-permute-start | bytes 221192 | tf_op jit(solution)/shard_map/ppermute | solution.py:51
  50.8 30.0 %copy-start.2 = (bf16[1,192,192]{2,1,0:T(8,128)(2,1)}, bf16[1,192,192]{2,1,0:T(8,128)(2,1)S(1)}, u32[]{:S(2)}) copy-start(bf16[1,192,192]{2,1,0:T(8,128)(2,1)S(1)} %collective-permute-done.3.after) | copy-start | bytes 221188
  50.8 30.0 %copy-start.3 = (bf16[1,192,192]{2,1,0:T(8,128)(2,1)}, bf16[1,192,192]{2,1,0:T(8,128)(2,1)S(1)}, u32[]{:S(2)}) copy-start(bf16[1,192,192]{2,1,0:T(8,128)(2,1)S(1)} %collective-permute-done.2.before) | copy-start | bytes 221188
  232.7 10.4 %collective-permute-start.5 = (f32[2,288,128]{2,1,0:T(8,128)S(1)}, f32[2,288,128]{2,1,0:T(8,128)S(1)}, u32[]{:S(2)}, u32[]{:S(2)}) collective-permute-start(f32[2,288,128]{2,1,0:T(8,128)S(1)} %get-tuple-element.7), channel_id=1, source_target_pairs={{1,0},{2,1},{3,2},{5,4},{6,5},{7,6},{9,8},{10,9},{11,10},{13,12},{... | collective-permute-start | bytes 884744 | tf_op jit(solution)/shard_map/ppermute | solution.py:51
  235.2 10.1 %collective-permute-start.4 = (f32[2,288,128]{2,1,0:T(8,128)S(1)}, f32[2,288,128]{2,1,0:T(8,128)S(1)}, u32[]{:S(2)}, u32[]{:S(2)}) collective-permute-start(f32[2,288,128]{2,1,0:T(8,128)S(1)} %get-tuple-element.8), channel_id=1, source_target_pairs={{0,1},{1,2},{2,3},{4,5},{5,6},{6,7},{8,9},{9,10},{10,11},{12,13},{... | collective-permute-start | bytes 884744 | tf_op jit(solution)/shard_map/ppermute | solution.py:51
  243.1 2.2 copy-start
  245.3 0.7 copy-start.1
Sparse Core Ops, SparseCore 0:
  37.5 43.3 all-gather.2
  119.0 112.5 all-reduce.7
